TPU v7x, 256 devices: a whole 4x4x8 slice. The times are simulated.
256 devices in a mesh: grp: 2 (over core), seq: 16 (over z, x_lo), head: 8 (over x_hi, y).
Axes of the slice: x: 4 (x_hi: 2, x_lo: 2; x = x_hi * 2 + x_lo), y: 4, z: 8, core: 2. Of those that a mesh axis runs over, the one named last changes fastest.
Arguments:
- patches: bfloat16 [4096, 1152], P(('grp', 'seq'), 'head'), may hold values from -200 to 200
- frames: int32 [4096], replicated, may hold values from 0 to 63, never falling along the last dimension, each value on 1 to 128 neighbouring positions
- enc_qkv: bfloat16 [3, 1152, 1152], P(None, None, 'head'), may hold values from -0.1875 to 0.1875
- enc_out: bfloat16 [1152, 1152], P('head'), may hold values from -0.1875 to 0.1875
- merge_gain: float32 [2, 4608], replicated, may hold values from 0.5 to 1.5
- merge_w: bfloat16 [2, 4608, 5120], P(None, ('grp', 'seq'), 'head'), may hold values from -0.09375 to 0.09375
- embedded: bfloat16 [8192, 5120], P(('grp', 'seq'), 'head'), may hold values from -200 to 200
- source: int32 [8192], P(('grp', 'seq')), may hold values from -1 to 1023, as said below
- dec_q: bfloat16 [5120, 4096], P(('grp', 'seq'), 'head'), may hold values from -0.078125 to 0.078125
- dec_kv: bfloat16 [5120, 2048], P(('grp', 'seq'), 'head'), may hold values from -0.078125 to 0.078125
- cotangent: bfloat16 [8192, 2, 5120], P(('grp', 'seq'), None, 'head'), may hold values from -6 to 6
Outputs:
- merged: bfloat16 [2, 1024, 5120], P(None, ('grp', 'seq'), 'head')
- context: bfloat16 [8192, 4096], P(('grp', 'seq'), 'head')
- level_grads: float32 [2, 1024, 5120], P(None, ('grp', 'seq'), 'head')
Inputs may be any that keep to these rules, and one draw needn't show every extreme that they name: `frames`: frame numbers never fall along the patches and no frame holds more than 128 patches. `source`: every merged token 0 to 1023 stands at exactly one position; all other positions hold -1; the rows of one device hold exactly 32 merged tokens, and at most 4 of those in one aligned block of 32 merged tokens, a most that some device reaches in every draw.
All inputs are finite; a program needn't handle non-finite values.
Results may differ from a plain program's by a relative error of at most 0.03.
The roundings to bfloat16 on the way count: a program that leaves them out, or rounds other values in their place, can miss the bound.
Values may be sent and summed in bfloat16 or wider, within the bound.
No kernel may reach another device: no remote copies, remote signals or barrier semaphores. Data moves between devices by JAX's collectives and lax.ppermute only.
A program may use at most 128 MiB of HBM per device.

v0:
```python
import jax
import jax.numpy as jnp
from jax import lax
from jax.sharding import PartitionSpec as P

ENC_HEADS = 16
HEAD_DIM = 128
RETURN_MOST = 4


def in_order(tiles, dim):
    shape = list(tiles.shape[1:])
    shape[dim] *= tiles.shape[0]
    return jnp.moveaxis(tiles, 0, dim).reshape(shape)


def from_everyone(value, axis):
    length = lax.axis_size(axis)
    return lax.all_to_all(
        jnp.broadcast_to(value[None], (length, *value.shape)), axis, 0, 0, tiled=True
    )


def gather_directly(value, axis, dim):
    return in_order(from_everyone(value, axis), dim)


def extended(value, sides, width):
    edges = {}
    for axis, dim in sides:
        size, length = (lax.axis_size(axis), value.shape[dim])
        up = [(i, (i + 1) % size) for i in range(size - 1)]
        last = lax.slice_in_dim(value, length - width, length, axis=dim)
        first = lax.slice_in_dim(value, 0, width, axis=dim)
        edges[dim] = (
            lax.ppermute(last, axis, up),
            lax.ppermute(first, axis, [(b, a) for a, b in up]),
        )
    done = []
    for _, dim in sides:
        low, high = edges[dim]
        around = [(width, width) if d in done else (0, 0) for d in range(value.ndim)]
        value = jnp.concatenate([jnp.pad(low, around), value, jnp.pad(high, around)], axis=dim)
        done.append(dim)
    return value


def in_blocks(value, dim, length):
    before, after = (value.shape[:dim], value.shape[dim + 1 :])
    return jnp.moveaxis(value.reshape(*before, length, -1, *after), dim, 0)


def summed_on_arrival(value, axis, dim):
    tiles = in_blocks(value, dim, lax.axis_size(axis))
    arrived = lax.all_to_all(tiles, axis, split_axis=0, concat_axis=0, tiled=True)
    return arrived.astype(jnp.float32).sum(axis=0)


def in_one_piece(arrays, axis, dim, along):
    ends, at = ([], 0)
    for a in arrays[:-1]:
        at += a.shape[along]
        ends.append(at)
    both = jnp.concatenate(arrays, axis=along)
    return tuple(jnp.split(lax.all_gather(both, axis, axis=dim, tiled=True), ends, axis=along))


def rms_rows(rows, gain):
    wide = rows.astype(jnp.float32)
    mean_sq = jnp.mean(wide * wide, axis=-1, keepdims=True)
    return wide * lax.rsqrt(mean_sq + 1e-06) * gain


def shards(
    patches,
    frames,
    enc_qkv,
    enc_out,
    merge_gain,
    merge_w,
    embedded,
    source,
    dec_q,
    dec_kv,
    cotangent,
):
    place = lax.axis_index(("grp", "seq"))
    pat_rows = patches.shape[0]
    full_patches = gather_directly(patches, "head", 1)
    enc_width = full_patches.shape[1]
    local_cols = enc_qkv.shape[2]
    enc_dim = enc_width // ENC_HEADS
    local_heads = local_cols // enc_dim
    enc_q = jnp.dot(full_patches, enc_qkv[0], preferred_element_type=jnp.float32).astype(
        jnp.bfloat16
    )
    enc_k = jnp.dot(full_patches, enc_qkv[1], preferred_element_type=jnp.float32).astype(
        jnp.bfloat16
    )
    enc_v = jnp.dot(full_patches, enc_qkv[2], preferred_element_type=jnp.float32).astype(
        jnp.bfloat16
    )
    paired = jnp.concatenate([enc_k, enc_v], axis=1)
    widened = extended(paired, ((("grp", "seq"), 0),), pat_rows)
    padded_frames = jnp.pad(frames, (pat_rows, pat_rows), constant_values=-1)
    key_frames = lax.dynamic_slice_in_dim(padded_frames, place * pat_rows, 3 * pat_rows)
    own_frames = lax.dynamic_slice_in_dim(frames, place * pat_rows, pat_rows)
    same = own_frames[:, None] == key_frames[None, :]
    query3 = enc_q.reshape(pat_rows, local_heads, enc_dim)
    keys3 = widened[:, :local_cols].reshape(3 * pat_rows, local_heads, enc_dim)
    values3 = widened[:, local_cols:].reshape(3 * pat_rows, local_heads, enc_dim)
    scores = jnp.einsum(
        "qhd,khd->hqk", query3, keys3, preferred_element_type=jnp.float32
    ) / jnp.sqrt(jnp.float32(enc_dim))
    scores = jnp.where(same[None], scores, jnp.float32(-1e30))
    top = jnp.max(scores, axis=2, keepdims=True)
    weights = jnp.where(same[None], jnp.exp(scores - top), jnp.float32(0.0))
    total = jnp.sum(weights, axis=2)
    mixed = jnp.einsum(
        "hqk,khd->qhd", weights.astype(jnp.bfloat16), values3, preferred_element_type=jnp.float32
    )
    enc_attn = (
        (mixed / jnp.transpose(total)[:, :, None])
        .astype(jnp.bfloat16)
        .reshape(pat_rows, local_cols)
    )
    partial_out = jnp.dot(enc_attn, enc_out, preferred_element_type=jnp.float32)
    summed = summed_on_arrival(partial_out.astype(jnp.bfloat16), "head", 1)
    enc_hidden = (patches.astype(jnp.float32) + summed).astype(jnp.bfloat16)
    full_hidden = gather_directly(enc_hidden, "head", 1)
    merged_rows = pat_rows // 4
    stacked = jnp.stack(
        [
            full_patches.reshape(merged_rows, 4 * enc_width),
            full_hidden.reshape(merged_rows, 4 * enc_width),
        ]
    )
    normed = rms_rows(stacked, merge_gain[:, None, :]).astype(jnp.bfloat16)
    block = normed
    merged = jnp.einsum(
        "lrk,lkc->lrc",
        block,
        lax.all_gather(merge_w, ("grp", "seq"), axis=1, tiled=True),
        preferred_element_type=jnp.float32,
    ).astype(jnp.bfloat16)
    tok_rows = embedded.shape[0]
    piece = lax.all_gather(merged[0], ("grp", "seq"), axis=0, tiled=True)
    picker = (source[:, None] == jnp.arange(piece.shape[0], dtype=jnp.int32)[None, :]).astype(
        jnp.bfloat16
    )
    inject = jnp.dot(picker, piece, preferred_element_type=jnp.float32)
    states = (embedded.astype(jnp.float32) + inject).astype(jnp.bfloat16)
    full_states = gather_directly(states, "head", 1)
    query_cols = dec_q.shape[1]
    pair_cols = dec_kv.shape[1]
    pieces = in_one_piece((dec_q, dec_kv), ("grp", "seq"), 0, 1)
    block = full_states
    query_sum = jnp.dot(block, pieces[0], preferred_element_type=jnp.float32)
    pair_sum = jnp.dot(block, pieces[1], preferred_element_type=jnp.float32)
    queries = query_sum.astype(jnp.bfloat16)
    keys_values = pair_sum.astype(jnp.bfloat16)
    kv_local = pair_cols // (2 * HEAD_DIM)
    group = query_cols // HEAD_DIM // kv_local
    query4 = queries.reshape(tok_rows, kv_local, group, HEAD_DIM)
    query_pos = place * tok_rows + jnp.arange(tok_rows, dtype=jnp.int32)
    scale = 1.0 / jnp.sqrt(jnp.float32(HEAD_DIM))
    piece = lax.all_gather(keys_values, ("grp", "seq"), axis=0, tiled=True)
    running_max = jnp.full((kv_local, group, tok_rows), -1e30, jnp.float32)
    count = piece.shape[0]
    split = piece.reshape(count, kv_local, 2, HEAD_DIM)
    keys = split[:, :, 0, :]
    values = split[:, :, 1, :]
    logits = jnp.einsum("qhgd,khd->hgqk", query4, keys, preferred_element_type=jnp.float32) * scale
    key_pos = jnp.arange(count, dtype=jnp.int32)
    visible = (query_pos[:, None] >= key_pos[None, :])[None, None]
    logits = jnp.where(visible, logits, jnp.float32(-1e30))
    new_max = jnp.maximum(running_max, jnp.max(logits, axis=3))
    probs = jnp.where(visible, jnp.exp(logits - new_max[..., None]), jnp.float32(0.0))
    new_sum = jnp.sum(probs, axis=3)
    new_accum = jnp.einsum(
        "hgqk,khd->hgqd", probs.astype(jnp.bfloat16), values, preferred_element_type=jnp.float32
    )
    normalized = (new_accum / new_sum[..., None]).astype(jnp.bfloat16)
    context = jnp.transpose(normalized, (2, 0, 1, 3)).reshape(tok_rows, query_cols)
    cot_flat = cotangent.reshape(tok_rows, 2 * cotangent.shape[2])
    holders = lax.axis_size(("grp", "seq"))
    capacity = RETURN_MOST
    visual = source >= 0
    holder = jnp.where(visual, source // merged_rows, -1)
    row_ids = jnp.arange(tok_rows, dtype=jnp.int32)
    earlier = (holder[:, None] == holder[None, :]) & (row_ids[None, :] < row_ids[:, None])
    order_rank = jnp.sum(earlier.astype(jnp.int32), axis=1)
    bucket_slot = jnp.where(visual, holder * capacity + order_rank, -1)
    placer = jnp.arange(holders * capacity, dtype=jnp.int32)[:, None] == bucket_slot[None, :]
    bucket_rows = jnp.dot(
        placer.astype(jnp.bfloat16), cot_flat, preferred_element_type=jnp.float32
    ).astype(jnp.bfloat16)
    bucket_ids = jnp.sum(jnp.where(placer, source[None, :] + 1, 0), axis=1) - 1
    arrived_rows, arrived_ids = (
        lax.all_to_all(bucket_rows, ("grp", "seq"), split_axis=0, concat_axis=0, tiled=True),
        lax.all_to_all(bucket_ids, ("grp", "seq"), split_axis=0, concat_axis=0, tiled=True),
    )
    local_index = arrived_ids - place * merged_rows
    setter = (jnp.arange(merged_rows, dtype=jnp.int32)[:, None] == local_index[None, :]).astype(
        jnp.bfloat16
    )
    returned = jnp.dot(setter, arrived_rows, preferred_element_type=jnp.float32)
    level_grads = jnp.transpose(returned.reshape(merged_rows, 2, cotangent.shape[2]), (1, 0, 2))
    return (merged, context, level_grads)


def solution(mesh):
    in_specs = (
        P(("grp", "seq"), "head"),
        P(),
        P(None, None, "head"),
        P("head", None),
        P(),
        P(None, ("grp", "seq"), "head"),
        P(("grp", "seq"), "head"),
        P(("grp", "seq")),
        P(("grp", "seq"), "head"),
        P(("grp", "seq"), "head"),
        P(("grp", "seq"), None, "head"),
    )
    out_specs = (
        P(None, ("grp", "seq"), "head"),
        P(("grp", "seq"), "head"),
        P(None, ("grp", "seq"), "head"),
    )
    return jax.shard_map(shards, mesh=mesh, in_specs=in_specs, out_specs=out_specs, check_vma=False)
```

profile of v0, /device:TPU:1, one launch (start us, length us, event | category | flops | bytes accessed | tf_op | source)
XLA Modules:
  0.0 407.7 jit_solution(7405874651068068960)
XLA Ops:
  7.2 0.7 all-gather.6.cloned.1.call-update
  7.9 1.5 broadcast_in_dim.55
  9.4 7.5 %all-to-all-start = ((bf16[8,128,144]{1,2,0:T(8,128)(2,1)}), bf16[8,128,144]{1,2,0:T(8,128)(2,1)S(1)}, u32[]{:S(2)}, u32[]{:S(2)}) async-start(bf16[8,128,144]{1,2,0:T(8,128)(2,1)} %broadcast_in_dim.55), calls=%async_computation | async-start | bytes 589824 | tf_op jit(solution)/shard_map/all_to_all | solution.py:19
  16.9 0.8 pad_dynamic-slice_fusion
  17.7 0.8 dynamic_slice.6
  18.4 0.1 broadcast_compare_fusion
  18.6 6.1 %all-to-all-done = bf16[8,128,144]{1,2,0:T(8,128)(2,1)S(1)} async-done(((bf16[8,128,144]{1,2,0:T(8,128)(2,1)}), bf16[8,128,144]{1,2,0:T(8,128)(2,1)S(1)}, u32[]{:S(2)}, u32[]{:S(2)}) %all-to-all-start) | async-done | bytes 294944 | tf_op jit(solution)/shard_map/all_to_all | solution.py:19
  24.6 1.2 convolution_convert_fusion.5
  25.9 1.2 convolution_convert_fusion.4
  27.1 9.7 %collective-permute-start.1 = (bf16[128,288]{0,1:T(8,128)(2,1)S(1)}, bf16[128,288]{0,1:T(8,128)(2,1)S(1)}, u32[]{:S(2)}, u32[]{:S(2)}) collective-permute-start(bf16[128,288]{0,1:T(8,128)(2,1)S(1)} %pad_maximum_fusion.4), channel_id=1, source_target_pairs={{8,0},{16,8},{24,16},{32,24},{40,32},{48,40},{56,48},{64,56},{72,6... | collective-permute-start | bytes 221192 | tf_op jit(solution)/shard_map/ppermute | solution.py:37
  36.8 1.9 collective-permute-start
  38.7 1.2 convolution_convert_fusion.3
  40.0 4.7 %collective-permute-done = bf16[128,288]{0,1:T(8,128)(2,1)S(1)} collective-permute-done((bf16[128,288]{0,1:T(8,128)(2,1)S(1)}, bf16[128,288]{0,1:T(8,128)(2,1)S(1)}, u32[]{:S(2)}, u32[]{:S(2)}) %collective-permute-start) | collective-permute-done | bytes 73760 | tf_op jit(solution)/shard_map/ppermute | solution.py:36
  44.7 0.4 fusion.79
  45.2 0.3 fusion.27
  45.4 0.3 fusion.39
  45.8 0.3 convolution_convert_fusion.1
  46.1 0.2 copy.44
  46.3 14.1 %all_to_all.38 = bf16[8,128,144]{1,2,0:T(8,128)(2,1)S(1)} all-to-all(bf16[8,128,144]{1,2,0:T(8,128)(2,1)S(1)} %bitcast.127), channel_id=1, replica_groups=mesh['grp'=2,'seq'=16,'head'=8] {'head'}, dimensions={0} | all-to-all | bytes 589824 | tf_op jit(solution)/shard_map/all_to_all | solution.py:55
  60.5 0.7 broadcast_in_dim.100
  61.2 3.4 all-to-all-start.2
  64.7 0.0 all-gather.12.cloned.1.call-start
  64.7 0.4 copy.43
  65.1 0.7 stack_reshape_reshape.6
  65.8 8.8 %all-to-all-done.2 = bf16[8,128,144]{1,2,0:T(8,128)(2,1)S(1)} async-done(((bf16[8,128,144]{1,2,0:T(8,128)(2,1)}), bf16[8,128,144]{1,2,0:T(8,128)(2,1)S(1)}, u32[]{:S(2)}, u32[]{:S(2)}) %all-to-all-start.2) | async-done | bytes 294944 | tf_op jit(solution)/shard_map/all_to_all | solution.py:19
  74.5 0.4 copy.45
  75.0 0.7 stack_reshape_reshape.7
  75.6 0.2 fusion.29
  75.9 21.8 %all-gather.6.cloned.1.call-done = bf16[2,4608,640]{2,1,0:T(8,128)(2,1)} async-done(((bf16[2,144,640]{2,1,0:T(8,128)(2,1)}), bf16[2,4608,640]{2,1,0:T(8,128)(2,1)}) %all-gather.6.cloned.1.call-update) | async-done | bytes 11796496 | tf_op jit(solution)/shard_map/all_gather | solution.py:143
  97.6 6.5 %convolution_convert_fusion.2 = bf16[2,32,640]{2,1,0:T(8,128)(2,1)S(1)} fusion(bf16[2,4608,640]{2,1,0:T(8,128)(2,1)} %all-gather.6.cloned.1.call-done, f32[2,4608]{1,0:T(2,128)S(1)} %copy-done.4, f32[2,32]{1,0:T(2,128)S(1)} %add_rsqrt_fusion, bf16[1,32,4608]{2,1,0:T(8,128)(2,1)S(1)} %stack_reshape_reshape.7, bf16[1,32,4608]{2,1,0:T(8,128)(2,1)S(1)} %stack_reshape_reshape.6), kind=kOutput, calls=%fused_computation.37 | convolution fusion | flops 379002880 | bytes 12505344 | tf_op jit(solution)/shard_map/lrk,lkc->lrc/dot_general | solution.py:140
  104.1 0.6 slice.34
  104.8 0.0 all-gather.8.cloned.1.call-start
  104.9 0.7 pad_maximum_fusion.2
  105.6 63.2 %all-gather.12.cloned.1.call-done = bf16[1,1024,640]{2,1,0:T(8,128)(2,1)} async-done(((bf16[1,32,640]{2,1,0:T(8,128)(2,1)}), bf16[1,1024,640]{2,1,0:T(8,128)(2,1)}) %all-gather.12.cloned.1.call-update) | async-done | bytes 1310736 | tf_op jit(solution)/shard_map/all_gather | solution.py:147
  168.8 1.9 fusion.20
  170.7 0.2 copy.46
  170.9 1.7 broadcast_in_dim.102
  172.6 6.1 %all-to-all-start.3 = ((bf16[8,256,640]{1,2,0:T(8,128)(2,1)}), bf16[8,256,640]{1,2,0:T(8,128)(2,1)S(1)}, u32[]{:S(2)}, u32[]{:S(2)}) async-start(bf16[8,256,640]{1,2,0:T(8,128)(2,1)} %broadcast_in_dim.102), calls=%async_computation.3 | async-start | bytes 5242880 | tf_op jit(solution)/shard_map/all_to_all | solution.py:19
  178.8 75.4 %all-gather.8.cloned.1.call-done = bf16[5120,768]{1,0:T(8,128)(2,1)} async-done(((bf16[160,768]{1,0:T(8,128)(2,1)}), bf16[5120,768]{1,0:T(8,128)(2,1)}) %all-gather.8.cloned.1.call-update) | async-done | bytes 7864336 | tf_op jit(solution)/shard_map/all_gather | solution.py:65
  254.2 4.2 %fusion.35 = bf16[256,256]{1,0:T(8,128)(2,1)} fusion(bf16[256,5120]{0,1:T(8,128)(2,1)S(1)} %bitcast.118, bf16[5120,768]{1,0:T(8,128)(2,1)} %all-gather.8.cloned.1.call-done), kind=kOutput, calls=%fused_computation.35 | convolution fusion | flops 671154176 | bytes 5373952 | tf_op jit(solution)/shard_map/dot_general | solution.py:159
  258.5 0.2 convert_reduce_fusion.1
  258.7 0.1 select_reduce_fusion
  258.8 0.7 sub.47
  259.5 6.4 %all-to-all-start.4 = ((s32[32,4,1]{1,2,0:T(1,128)}), s32[32,4,1]{1,2,0:T(1,128)S(1)}, u32[]{:S(2)}, u32[]{:S(2)}) async-start(s32[32,4,1]{1,2,0:T(1,128)} %bitcast.29), calls=%async_computation.4 | async-start | bytes 32768 | tf_op jit(solution)/shard_map/all_to_all | solution.py:201
  266.0 1.2 copy.58
  267.1 0.3 convolution_convert_fusion
  267.4 0.8 all_to_all.29
  268.2 5.5 %all-to-all-done.4 = s32[32,4,1]{1,2,0:T(1,128)S(1)} async-done(((s32[32,4,1]{1,2,0:T(1,128)}), s32[32,4,1]{1,2,0:T(1,128)S(1)}, u32[]{:S(2)}, u32[]{:S(2)}) %all-to-all-start.4) | async-done | bytes 544 | tf_op jit(solution)/shard_map/all_to_all | solution.py:201
  273.7 4.4 %all-to-all-start.5 = ((bf16[32,4,1280]{2,1,0:T(4,128)(2,1)}), bf16[32,4,1280]{2,1,0:T(4,128)(2,1)S(1)}, u32[]{:S(2)}, u32[]{:S(2)}) async-start(bf16[32,4,1280]{2,1,0:T(4,128)(2,1)} %all_to_all.29), calls=%async_computation.5 | async-start | bytes 655360 | tf_op jit(solution)/shard_map/all_to_all | solution.py:200
  278.1 1.4 iota_compare_fusion
  279.6 0.1 sub.50
  279.7 14.1 %all-to-all-done.5 = bf16[32,4,1280]{2,1,0:T(4,128)(2,1)S(1)} async-done(((bf16[32,4,1280]{2,1,0:T(4,128)(2,1)}), bf16[32,4,1280]{2,1,0:T(4,128)(2,1)S(1)}, u32[]{:S(2)}, u32[]{:S(2)}) %all-to-all-start.5) | async-done | bytes 327712 | tf_op jit(solution)/shard_map/all_to_all | solution.py:200
  293.8 0.1 all_to_all.31
  293.9 0.2 copy.52
  294.1 0.9 convolution_bitcast_fusion
  295.0 4.9 %fusion.32 = bf16[32,4,8,128]{3,2,1,0:T(8,128)(2,1)S(1)} fusion(bf16[256,5120]{0,1:T(8,128)(2,1)} %bitcast.119, bf16[5120,768]{1,0:T(8,128)(2,1)} %all-gather.8.cloned.1.call-done), kind=kOutput, calls=%fused_computation.34 | convolution fusion | flops 1342308352 | bytes 8126464 | tf_op jit(solution)/shard_map/dot_general | solution.py:158
  299.9 28.8 %all-gather.10.cloned.1.call-done = bf16[8192,256]{1,0:T(8,128)(2,1)} async-done(((bf16[256,256]{1,0:T(8,128)(2,1)}), bf16[8192,256]{1,0:T(8,128)(2,1)}) %all-gather.10.cloned.1.call-update) | async-done | bytes 4194320 | tf_op jit(solution)/shard_map/all_gather | solution.py:167
  328.7 6.9 %reshape.176 = bf16[8192,1,2,128]{3,2,0,1:T(2,128)(2,1)} reshape(bf16[8192,256]{1,0:T(8,128)(2,1)} %all-gather.10.cloned.1.call-done) | data formatting | bytes 8388608 | tf_op jit(solution)/shard_map/reshape | solution.py:170
  335.6 10.0 %fusion.77 = (bf16[8192,1,1,128]{3,2,0,1:T(2,128)(2,1)}, bf16[8192,1,1,128]{3,2,0,1:T(2,128)(2,1)}) fusion(bf16[8192,1,2,128]{3,2,0,1:T(2,128)(2,1)} %reshape.176), kind=kLoop, calls=%fused_computation.97 | loop fusion | bytes 8388608 | tf_op jit(solution)/shard_map/slice | solution.py:172
  345.6 9.2 %copy.55 = bf16[8192,1,1,128]{0,3,2,1:T(8,128)(2,1)} copy(bf16[8192,1,1,128]{3,2,0,1:T(2,128)(2,1)} %get-tuple-element.15) | data formatting | bytes 4194304
  354.8 15.5 %fusion.1 = (f32[4,256]{1,0:T(4,128)S(1)}, f32[8192,256,4]{1,0,2:T(8,128)}) fusion(pred[256,8192]{0,1:T(8,128)(4,1)S(1)} %iota_compare_fusion, bf16[32,4,8,128]{3,2,1,0:T(8,128)(2,1)S(1)} %fusion.32, bf16[8192,1,1,128]{3,2,0,1:T(2,128)(2,1)} %get-tuple-element.16), kind=kOutput, calls=%fused_computation.3 | convolution fusion | flops 2172648448 | bytes 38014976 | tf_op jit(solution)/shard_map/qhgd,khd->hgqk/dot_general | solution.py:173
  370.3 15.0 %fusion.2 = f32[4,256]{1,0:T(4,128)S(1)} fusion(f32[8192,256,4]{1,0,2:T(8,128)} %get-tuple-element.22, f32[4,256]{1,0:T(4,128)S(1)} %broadcast_maximum_fusion, pred[256,8192]{0,1:T(8,128)(4,1)S(1)} %iota_compare_fusion), kind=kLoop, calls=%fused_computation.4 | loop fusion | flops 41942016 | bytes 35659776 | tf_op jit(solution)/shard_map/reduce_sum | solution.py:179
  385.4 15.0 %fusion.45 = bf16[4,256,128]{1,2,0:T(8,128)(2,1)S(1)} fusion(f32[8192,256,4]{1,0,2:T(8,128)} %get-tuple-element.22, f32[4,256]{1,0:T(4,128)S(1)} %broadcast_maximum_fusion, pred[256,8192]{0,1:T(8,128)(4,1)S(1)} %iota_compare_fusion, bf16[8192,1,1,128]{0,3,2,1:T(8,128)(2,1)} %copy.55, f32[4,256]{1,0:T(4,128)S(1)} %fusion.2), kind=kOutput, calls=%fused_computation.46 | convolution fusion | flops 2189688832 | bytes 38019072 | tf_op jit(solution)/shard_map/hgqk,khd->hgqd/dot_general | solution.py:180
  400.4 0.8 copy.53
  (39 shorter events, 0.4 us)
Async XLA Ops:
  7.2 38.6 %copy-start = (bf16[144,1152]{1,0:T(8,128)(2,1)S(1)}, bf16[144,1152]{1,0:T(8,128)(2,1)}, u32[]{:S(2)}) copy-start(bf16[144,1152]{1,0:T(8,128)(2,1)} %param.14) | copy-start | bytes 995332
  7.2 53.3 %copy-start.6 = (bf16[128,144]{0,1:T(8,128)(2,1)S(1)}, bf16[128,144]{0,1:T(8,128)(2,1)}, u32[]{:S(2)}) copy-start(bf16[128,144]{0,1:T(8,128)(2,1)} %param.11) | copy-start | bytes 110596
  7.2 90.4 %all-gather.6.cloned.1.call-start = ((), (), s32[]{:S(2)}) async-start(), calls=%async_computation.6 | async-start | bytes 12165120 | tf_op jit(solution)/shard_map/all_gather | solution.py:143
  9.4 15.2 %all-to-all-start = ((bf16[8,128,144]{1,2,0:T(8,128)(2,1)}), bf16[8,128,144]{1,2,0:T(8,128)(2,1)S(1)}, u32[]{:S(2)}, u32[]{:S(2)}) async-start(bf16[8,128,144]{1,2,0:T(8,128)(2,1)} %broadcast_in_dim.55), calls=%async_computation | async-start | bytes 589824 | tf_op jit(solution)/shard_map/all_to_all | solution.py:19
  27.1 12.9 %collective-permute-start.1 = (bf16[128,288]{0,1:T(8,128)(2,1)S(1)}, bf16[128,288]{0,1:T(8,128)(2,1)S(1)}, u32[]{:S(2)}, u32[]{:S(2)}) collective-permute-start(bf16[128,288]{0,1:T(8,128)(2,1)S(1)} %pad_maximum_fusion.4), channel_id=1, source_target_pairs={{8,0},{16,8},{24,16},{32,24},{40,32},{48,40},{56,48},{64,56},{72,6... | collective-permute-start | bytes 221192 | tf_op jit(solution)/shard_map/ppermute | solution.py:37
  36.8 7.9 %collective-permute-start = (bf16[128,288]{0,1:T(8,128)(2,1)S(1)}, bf16[128,288]{0,1:T(8,128)(2,1)S(1)}, u32[]{:S(2)}, u32[]{:S(2)}) collective-permute-start(bf16[128,288]{0,1:T(8,128)(2,1)S(1)} %pad_maximum_fusion.4), channel_id=1, source_target_pairs={{0,8},{8,16},{16,24},{24,32},{32,40},{40,48},{48,56},{56,64},{64,7... | collective-permute-start | bytes 221192 | tf_op jit(solution)/shard_map/ppermute | solution.py:36
  40.0 57.7 %copy-start.4 = (f32[2,4608]{1,0:T(2,128)S(1)}, f32[2,4608]{1,0:T(2,128)}, u32[]{:S(2)}) copy-start(f32[2,4608]{1,0:T(2,128)} %param.15) | copy-start | bytes 110596
  61.2 13.3 %all-to-all-start.2 = ((bf16[8,128,144]{1,2,0:T(8,128)(2,1)}), bf16[8,128,144]{1,2,0:T(8,128)(2,1)S(1)}, u32[]{:S(2)}, u32[]{:S(2)}) async-start(bf16[8,128,144]{1,2,0:T(8,128)(2,1)} %broadcast_in_dim.100), calls=%async_computation.2 | async-start | bytes 589824 | tf_op jit(solution)/shard_map/all_to_all | solution.py:19
  64.7 104.1 %all-gather.12.cloned.1.call-start = ((), (), s32[]{:S(2)}) async-start(), calls=%async_computation.9 | async-start | bytes 1351680 | tf_op jit(solution)/shard_map/all_gather | solution.py:147
  75.8 29.0 %copy-start.5 = (bf16[160,512]{1,0:T(8,128)(2,1)S(1)}, bf16[160,512]{1,0:T(8,128)(2,1)}, u32[]{:S(2)}) copy-start(bf16[160,512]{1,0:T(8,128)(2,1)} %param.19) | copy-start | bytes 491524
  75.8 29.0 %copy-start.7 = (bf16[160,256]{1,0:T(8,128)(2,1)S(1)}, bf16[160,256]{1,0:T(8,128)(2,1)}, u32[]{:S(2)}) copy-start(bf16[160,256]{1,0:T(8,128)(2,1)} %param.20) | copy-start | bytes 245764
  75.8 92.9 %copy-start.8 = (s32[256]{0:T(256)S(1)}, s32[256]{0:T(256)}, u32[]{:S(2)}) copy-start(s32[256]{0:T(256)} %param.18) | copy-start | bytes 3076
  75.9 92.9 %copy-start.9 = (bf16[256,640]{1,0:T(8,128)(2,1)S(1)}, bf16[256,640]{1,0:T(8,128)(2,1)}, u32[]{:S(2)}) copy-start(bf16[256,640]{1,0:T(8,128)(2,1)} %param.17) | copy-start | bytes 983044
  104.1 68.5 %copy-start.3 = (bf16[2,32,640]{2,1,0:T(8,128)(2,1)}, bf16[2,32,640]{2,1,0:T(8,128)(2,1)S(1)}, u32[]{:S(2)}) copy-start(bf16[2,32,640]{2,1,0:T(8,128)(2,1)S(1)} %convolution_convert_fusion.2) | copy-start | bytes 245764
  104.8 149.4 %all-gather.8.cloned.1.call-start = ((), (), s32[]{:S(2)}) async-start(), calls=%async_computation.7 | async-start | bytes 8110080 | tf_op jit(solution)/shard_map/all_gather | solution.py:65
  172.6 81.6 %all-to-all-start.3 = ((bf16[8,256,640]{1,2,0:T(8,128)(2,1)}), bf16[8,256,640]{1,2,0:T(8,128)(2,1)S(1)}, u32[]{:S(2)}, u32[]{:S(2)}) async-start(bf16[8,256,640]{1,2,0:T(8,128)(2,1)} %broadcast_in_dim.102), calls=%async_computation.3 | async-start | bytes 5242880 | tf_op jit(solution)/shard_map/all_to_all | solution.py:19
  178.8 149.9 %all-gather.10.cloned.1.call-start = ((), (), s32[]{:S(2)}) async-start(), calls=%async_computation.8 | async-start | bytes 4325376 | tf_op jit(solution)/shard_map/all_gather | solution.py:167
  254.2 13.2 %copy-start.2 = (bf16[8,256,640]{1,2,0:T(8,128)(2,1)}, bf16[8,256,640]{1,2,0:T(8,128)(2,1)S(1)}, u32[]{:S(2)}) copy-start(bf16[8,256,640]{1,2,0:T(8,128)(2,1)S(1)} %all-to-all-done.3) | copy-start | bytes 7864324
  259.5 14.2 %all-to-all-start.4 = ((s32[32,4,1]{1,2,0:T(1,128)}), s32[32,4,1]{1,2,0:T(1,128)S(1)}, u32[]{:S(2)}, u32[]{:S(2)}) async-start(s32[32,4,1]{1,2,0:T(1,128)} %bitcast.29), calls=%async_computation.4 | async-start | bytes 32768 | tf_op jit(solution)/shard_map/all_to_all | solution.py:201
  273.7 20.1 %all-to-all-start.5 = ((bf16[32,4,1280]{2,1,0:T(4,128)(2,1)}), bf16[32,4,1280]{2,1,0:T(4,128)(2,1)S(1)}, u32[]{:S(2)}, u32[]{:S(2)}) async-start(bf16[32,4,1280]{2,1,0:T(4,128)(2,1)} %all_to_all.29), calls=%async_computation.5 | async-start | bytes 655360 | tf_op jit(solution)/shard_map/all_to_all | solution.py:200
  385.3 15.9 %copy-start.1 = (bf16[144,1152]{1,0:T(8,128)(2,1)S(1)}, bf16[144,1152]{1,0:T(8,128)(2,1)}, u32[]{:S(2)}) copy-start(bf16[144,1152]{1,0:T(8,128)(2,1)} %param.14) | copy-start | bytes 995332
Sparse Core Ops, SparseCore 0:
  9.9 87.7 all-gather.5
  104.9 63.8 all-gather.11
  171.2 82.9 all-gather.7
  258.6 70.0 all-gather.9
where the time goes:
time: 409 us; the launch traced here: 408 us
  waiting for transfers between devices  229 us (56%)
  matrix products  54.2 us (13%)
  starting transfers between devices  39.5 us (10%)
  local copies, waits for them, and re-layouts  38.8 us (9%)
  other arithmetic  17.9 us (4%)
  blocking collectives  14.1 us (3%)
  between operations  14.1 us (3%)
    all_gather x1, waiting for transfers between devices, in_one_piece(): lax.all_gather(both, axis, axis=dim, tiled=True)  75.4 us
    all_gather x1, waiting for transfers between devices, shards(): piece = lax.all_gather(merged[0], ('grp', 'seq'), axis=0, tiled=True)  63.2 us
    all_gather x1, waiting for transfers between devices, shards(): piece = lax.all_gather(keys_values, ('grp', 'seq'), axis=0, tiled=True)  28.8 us
    all_gather x1, waiting for transfers between devices, shards(): lax.all_gather(merge_w, ('grp', 'seq'), axis=1, tiled=True)  21.8 us
    all_to_all x3, starting transfers between devices, from_everyone(): lax.all_to_all(jnp.broadcast_to(value[None], (length, *value.shape)), axi...  17 us
    dot_general x1, matrix products, shards(): jnp.einsum('qhgd,khd->hgqk', query4, keys, preferred_element_type=jnp.flo...  15.5 us
    reduce_sum x1, other arithmetic, shards(): new_sum = jnp.sum(probs, axis=3)  15 us
    dot_general x1, matrix products, shards(): jnp.einsum('hgqk,khd->hgqd', probs.astype(jnp.bfloat16), values, preferre...  15 us
  transfers between devices with their start and end apart: 11, of which 9 were waited for; matrix products, arithmetic and copies ran while one was open for 6% of the time, Pallas kernels for 0%

commit v1 on v0

--- a/solution.py
+++ b/solution.py
@@ -137,10 +137,22 @@
     )
     normed = rms_rows(stacked, merge_gain[:, None, :]).astype(jnp.bfloat16)
     block = normed
+
+    def detail_sector(obj, a_name):
+        return jnp.concatenate(
+            lax.all_to_all(
+                jnp.stack([obj] * lax.axis_size(a_name), axis=0),
+                a_name,
+                split_axis=0,
+                concat_axis=0,
+            ),
+            axis=1,
+        )
+
     merged = jnp.einsum(
         "lrk,lkc->lrc",
         block,
-        lax.all_gather(merge_w, ("grp", "seq"), axis=1, tiled=True),
+        detail_sector(merge_w, ("grp", "seq")),
         preferred_element_type=jnp.float32,
     ).astype(jnp.bfloat16)
     tok_rows = embedded.shape[0]

time: 409 us -> 659 us (1.61)
  waiting for transfers between devices: 229 us -> 462 us
  local copies, waits for them, and re-layouts: 38.8 us -> 49.2 us
  blocking collectives: 14.1 us -> 21.4 us
    all_to_all x0 -> x1, waiting for transfers between devices: none -> 255 us  [detail_sector(): lax.all_to_all(jnp.stack([obj] * lax.axis_size(a_name), axis=0), a_name,...]
    all_gather x1 -> x0, waiting for transfers between devices: 21.8 us -> none  [shards(): lax.all_gather(merge_w, ('grp', 'seq'), axis=1, tiled=True)]
    all_to_all x0 -> x1, blocking collectives: none -> 10.4 us  [from_everyone(): lax.all_to_all(jnp.broadcast_to(value[None], (length, *value.shape)), axi...]
    all_gather x1, waiting for transfers between devices: 63.2 us -> 72.3 us  [shards(): piece = lax.all_gather(merged[0], ('grp', 'seq'), axis=0, tiled=True)]
    all_to_all x3 -> x2, waiting for transfers between devices: 14.9 us -> 6.07 us  [from_everyone(): lax.all_to_all(jnp.broadcast_to(value[None], (length, *value.shape)), axi...]
    all_to_all x3 -> x2, starting transfers between devices: 17 us -> 13.6 us  [from_everyone(): lax.all_to_all(jnp.broadcast_to(value[None], (length, *value.shape)), axi...]
  transfers between devices with their start and end apart: 11 -> 10, of which waited for: 9 -> 8; matrix products, arithmetic and copies ran while one was open for 6% -> 3% of each run, Pallas kernels for 0% -> 0%
where the time goes in v1:
time: 659 us; the launch traced here: 657 us
  waiting for transfers between devices  462 us (70%)
  matrix products  49.9 us (8%)
  local copies, waits for them, and re-layouts  49.2 us (7%)
  starting transfers between devices  42.6 us (6%)
  blocking collectives  21.4 us (3%)
  other arithmetic  17.9 us (3%)
  between operations  14.1 us (2%)
    all_to_all x1, waiting for transfers between devices, detail_sector(): lax.all_to_all(jnp.stack([obj] * lax.axis_size(a_name), axis=0), a_name,...  255 us
    all_gather x1, waiting for transfers between devices, in_one_piece(): lax.all_gather(both, axis, axis=dim, tiled=True)  75.4 us
    all_gather x1, waiting for transfers between devices, shards(): piece = lax.all_gather(merged[0], ('grp', 'seq'), axis=0, tiled=True)  72.3 us
    all_gather x1, waiting for transfers between devices, shards(): piece = lax.all_gather(keys_values, ('grp', 'seq'), axis=0, tiled=True)  29 us
    dot_general x1, matrix products, shards(): jnp.einsum('qhgd,khd->hgqk', query4, keys, preferred_element_type=jnp.flo...  15.5 us
    reduce_sum x1, other arithmetic, shards(): new_sum = jnp.sum(probs, axis=3)  15 us
    dot_general x1, matrix products, shards(): jnp.einsum('hgqk,khd->hgqd', probs.astype(jnp.bfloat16), values, preferre...  15 us
    all_to_all x1, waiting for transfers between devices, shards(): lax.all_to_all(bucket_rows, ('grp', 'seq'), split_axis=0, concat_axis=0,...  14.1 us
  transfers between devices with their start and end apart: 10, of which 8 were waited for; matrix products, arithmetic and copies ran while one was open for 3% of the time, Pallas kernels for 0%

profile of v1, /device:TPU:1, one launch (start us, length us, event | category | flops | bytes accessed | tf_op | source)
XLA Modules:
  0.0 657.1 jit_solution(6125903520941959538)
XLA Ops:
  7.2 1.6 broadcast_in_dim.55
  8.8 7.5 %all-to-all-start = ((bf16[8,128,144]{1,2,0:T(8,128)(2,1)}), bf16[8,128,144]{1,2,0:T(8,128)(2,1)S(1)}, u32[]{:S(2)}, u32[]{:S(2)}) async-start(bf16[8,128,144]{1,2,0:T(8,128)(2,1)} %broadcast_in_dim.55), calls=%async_computation | async-start | bytes 589824 | tf_op jit(solution)/shard_map/all_to_all | solution.py:19
  16.2 0.8 pad_dynamic-slice_fusion
  17.0 0.8 dynamic_slice.6
  17.8 0.1 broadcast_compare_fusion
  17.9 6.1 all-to-all-done
  24.0 1.2 convolution_convert_fusion.5
  25.2 1.2 convolution_convert_fusion.4
  26.4 9.7 %collective-permute-start.1 = (bf16[128,288]{0,1:T(8,128)(2,1)S(1)}, bf16[128,288]{0,1:T(8,128)(2,1)S(1)}, u32[]{:S(2)}, u32[]{:S(2)}) collective-permute-start(bf16[128,288]{0,1:T(8,128)(2,1)S(1)} %pad_maximum_fusion.4), channel_id=1, source_target_pairs={{8,0},{16,8},{24,16},{32,24},{40,32},{48,40},{56,48},{64,56},{72,6... | collective-permute-start | bytes 221192 | tf_op jit(solution)/shard_map/ppermute | solution.py:37
  36.1 1.9 collective-permute-start
  38.1 1.2 convolution_convert_fusion.3
  39.3 4.6 collective-permute-done
  44.0 0.4 fusion.79
  44.4 0.3 fusion.27
  44.7 0.3 fusion.39
  45.0 0.3 convolution_convert_fusion.1
  45.3 0.2 copy.45
  45.5 11.0 %all_to_all.43 = bf16[8,128,144]{1,2,0:T(8,128)(2,1)S(1)} all-to-all(bf16[8,128,144]{1,2,0:T(8,128)(2,1)S(1)} %bitcast.130), channel_id=1, replica_groups=mesh['grp'=2,'seq'=16,'head'=8] {'head'}, dimensions={0} | all-to-all | bytes 589824 | tf_op jit(solution)/shard_map/all_to_all | solution.py:55
  56.6 10.4 %all_to_all.44 = bf16[8,128,144]{1,2,0:T(8,128)(2,1)S(1)} all-to-all(bf16[8,128,144]{1,2,0:T(8,128)(2,1)S(1)} %broadcast_in_dim.100), channel_id=1, replica_groups=mesh['grp'=2,'seq'=16,'head'=8] {'head'}, dimensions={0} | all-to-all | bytes 589824 | tf_op jit(solution)/shard_map/all_to_all | solution.py:19
  67.0 5.2 stack.5
  72.2 6.5 all-to-all-start.3
  78.7 0.0 all-gather.9.cloned.1.call-start
  78.7 0.4 copy.44
  79.1 0.7 stack_reshape_reshape.6
  79.8 0.4 copy.46
  80.2 0.7 stack_reshape_reshape.7
  80.9 0.2 fusion.29
  81.1 255.0 %all-to-all-done.3 = bf16[32,2,144,640]{3,2,1,0:T(8,128)(2,1)} async-done(((bf16[32,2,144,640]{3,2,1,0:T(8,128)(2,1)}), bf16[32,2,144,640]{3,2,1,0:T(8,128)(2,1)}, u32[]{:S(2)}, u32[]{:S(2)}) %all-to-all-start.3) | async-done | bytes 11796512 | tf_op jit(solution)/shard_map/all_to_all | solution.py:143
  336.1 6.0 copy.47
  342.2 2.1 convolution_convert_fusion.2
  344.4 0.6 slice.34
  345.0 0.0 all-gather.5.cloned.1.call-start
  345.1 0.7 pad_maximum_fusion.2
  345.8 72.3 %all-gather.9.cloned.1.call-done = bf16[1,1024,640]{2,1,0:T(8,128)(2,1)} async-done(((bf16[1,32,640]{2,1,0:T(8,128)(2,1)}), bf16[1,1024,640]{2,1,0:T(8,128)(2,1)}) %all-gather.9.cloned.1.call-update) | async-done | bytes 1310736 | tf_op jit(solution)/shard_map/all_gather | solution.py:159
  418.1 1.9 fusion.20
  420.0 0.2 copy.48
  420.2 1.7 broadcast_in_dim.102
  422.0 6.1 all-to-all-start.4
  428.1 75.4 %all-gather.5.cloned.1.call-done = bf16[5120,768]{1,0:T(8,128)(2,1)} async-done(((bf16[160,768]{1,0:T(8,128)(2,1)}), bf16[5120,768]{1,0:T(8,128)(2,1)}) %all-gather.5.cloned.1.call-update) | async-done | bytes 7864336 | tf_op jit(solution)/shard_map/all_gather | solution.py:65
  503.5 4.2 fusion.35
  507.8 0.2 convert_reduce_fusion.1
  508.0 0.1 select_reduce_fusion
  508.1 0.7 sub.47
  508.8 6.4 all-to-all-start.5
  515.3 1.2 copy.60
  516.4 0.3 convolution_convert_fusion
  516.7 0.8 all_to_all.33
  517.5 5.5 all-to-all-done.5
  523.0 4.4 all-to-all-start.6
  527.4 1.4 iota_compare_fusion
  528.9 0.1 sub.50
  529.0 14.1 %all-to-all-done.6 = bf16[32,4,1280]{2,1,0:T(4,128)(2,1)S(1)} async-done(((bf16[32,4,1280]{2,1,0:T(4,128)(2,1)}), bf16[32,4,1280]{2,1,0:T(4,128)(2,1)S(1)}, u32[]{:S(2)}, u32[]{:S(2)}) %all-to-all-start.6) | async-done | bytes 327712 | tf_op jit(solution)/shard_map/all_to_all | solution.py:212
  543.1 0.1 all_to_all.35
  543.2 0.2 copy.54
  543.4 0.9 convolution_bitcast_fusion
  544.3 4.9 fusion.32
  549.2 29.0 %all-gather.7.cloned.1.call-done = bf16[8192,256]{1,0:T(8,128)(2,1)} async-done(((bf16[256,256]{1,0:T(8,128)(2,1)}), bf16[8192,256]{1,0:T(8,128)(2,1)}) %all-gather.7.cloned.1.call-update) | async-done | bytes 4194320 | tf_op jit(solution)/shard_map/all_gather | solution.py:179
  578.1 6.9 %reshape.186 = bf16[8192,1,2,128]{3,2,0,1:T(2,128)(2,1)} reshape(bf16[8192,256]{1,0:T(8,128)(2,1)} %all-gather.7.cloned.1.call-done) | data formatting | bytes 8388608 | tf_op jit(solution)/shard_map/reshape | solution.py:182
  585.0 9.9 %fusion.77 = (bf16[8192,1,1,128]{3,2,0,1:T(2,128)(2,1)}, bf16[8192,1,1,128]{3,2,0,1:T(2,128)(2,1)}) fusion(bf16[8192,1,2,128]{3,2,0,1:T(2,128)(2,1)} %reshape.186), kind=kLoop, calls=%fused_computation.97 | loop fusion | bytes 8388608 | tf_op jit(solution)/shard_map/slice | solution.py:184
  594.9 9.2 %copy.57 = bf16[8192,1,1,128]{0,3,2,1:T(8,128)(2,1)} copy(bf16[8192,1,1,128]{3,2,0,1:T(2,128)(2,1)} %get-tuple-element.15) | data formatting | bytes 4194304
  604.1 15.5 %fusion.1 = (f32[4,256]{1,0:T(4,128)S(1)}, f32[8192,256,4]{1,0,2:T(8,128)}) fusion(pred[256,8192]{0,1:T(8,128)(4,1)S(1)} %iota_compare_fusion, bf16[32,4,8,128]{3,2,1,0:T(8,128)(2,1)S(1)} %fusion.32, bf16[8192,1,1,128]{3,2,0,1:T(2,128)(2,1)} %get-tuple-element.16), kind=kOutput, calls=%fused_computation.3 | convolution fusion | flops 2172648448 | bytes 38014976 | tf_op jit(solution)/shard_map/qhgd,khd->hgqk/dot_general | solution.py:185
  619.6 15.0 %fusion.2 = f32[4,256]{1,0:T(4,128)S(1)} fusion(f32[8192,256,4]{1,0,2:T(8,128)} %get-tuple-element.22, f32[4,256]{1,0:T(4,128)S(1)} %broadcast_maximum_fusion, pred[256,8192]{0,1:T(8,128)(4,1)S(1)} %iota_compare_fusion), kind=kLoop, calls=%fused_computation.4 | loop fusion | flops 41942016 | bytes 35659776 | tf_op jit(solution)/shard_map/reduce_sum | solution.py:191
  634.7 15.0 %fusion.45 = bf16[4,256,128]{1,2,0:T(8,128)(2,1)S(1)} fusion(f32[8192,256,4]{1,0,2:T(8,128)} %get-tuple-element.22, f32[4,256]{1,0:T(4,128)S(1)} %broadcast_maximum_fusion, pred[256,8192]{0,1:T(8,128)(4,1)S(1)} %iota_compare_fusion, bf16[8192,1,1,128]{0,3,2,1:T(8,128)(2,1)} %copy.57, f32[4,256]{1,0:T(4,128)S(1)} %fusion.2), kind=kOutput, calls=%fused_computation.46 | convolution fusion | flops 2189688832 | bytes 38019072 | tf_op jit(solution)/shard_map/hgqk,khd->hgqd/dot_general | solution.py:192
  649.7 0.8 copy.55
  (41 shorter events, 0.4 us)
Async XLA Ops:
  7.2 37.8 %copy-start = (bf16[144,1152]{1,0:T(8,128)(2,1)S(1)}, bf16[144,1152]{1,0:T(8,128)(2,1)}, u32[]{:S(2)}) copy-start(bf16[144,1152]{1,0:T(8,128)(2,1)} %param.14) | copy-start | bytes 995332
  7.2 49.4 %copy-start.7 = (bf16[128,144]{0,1:T(8,128)(2,1)S(1)}, bf16[128,144]{0,1:T(8,128)(2,1)}, u32[]{:S(2)}) copy-start(bf16[128,144]{0,1:T(8,128)(2,1)} %param.11) | copy-start | bytes 110596
  7.2 59.8 %copy-start.5 = (bf16[2,144,640]{2,1,0:T(8,128)(2,1)S(1)}, bf16[2,144,640]{2,1,0:T(8,128)(2,1)}, u32[]{:S(2)}) copy-start(bf16[2,144,640]{2,1,0:T(8,128)(2,1)} %param.16) | copy-start | bytes 1105924
  8.8 15.2 %all-to-all-start = ((bf16[8,128,144]{1,2,0:T(8,128)(2,1)}), bf16[8,128,144]{1,2,0:T(8,128)(2,1)S(1)}, u32[]{:S(2)}, u32[]{:S(2)}) async-start(bf16[8,128,144]{1,2,0:T(8,128)(2,1)} %broadcast_in_dim.55), calls=%async_computation | async-start | bytes 589824 | tf_op jit(solution)/shard_map/all_to_all | solution.py:19
  26.4 12.9 %collective-permute-start.1 = (bf16[128,288]{0,1:T(8,128)(2,1)S(1)}, bf16[128,288]{0,1:T(8,128)(2,1)S(1)}, u32[]{:S(2)}, u32[]{:S(2)}) collective-permute-start(bf16[128,288]{0,1:T(8,128)(2,1)S(1)} %pad_maximum_fusion.4), channel_id=1, source_target_pairs={{8,0},{16,8},{24,16},{32,24},{40,32},{48,40},{56,48},{64,56},{72,6... | collective-permute-start | bytes 221192 | tf_op jit(solution)/shard_map/ppermute | solution.py:37
  36.1 7.8 %collective-permute-start = (bf16[128,288]{0,1:T(8,128)(2,1)S(1)}, bf16[128,288]{0,1:T(8,128)(2,1)S(1)}, u32[]{:S(2)}, u32[]{:S(2)}) collective-permute-start(bf16[128,288]{0,1:T(8,128)(2,1)S(1)} %pad_maximum_fusion.4), channel_id=1, source_target_pairs={{0,8},{8,16},{16,24},{24,32},{32,40},{40,48},{48,56},{56,64},{64,7... | collective-permute-start | bytes 221192 | tf_op jit(solution)/shard_map/ppermute | solution.py:36
  72.2 263.9 %all-to-all-start.3 = ((bf16[32,2,144,640]{3,2,1,0:T(8,128)(2,1)}), bf16[32,2,144,640]{3,2,1,0:T(8,128)(2,1)}, u32[]{:S(2)}, u32[]{:S(2)}) async-start(bf16[32,2,144,640]{3,2,1,0:T(8,128)(2,1)} %stack.5), calls=%async_computation.3 | async-start | bytes 23592960 | tf_op jit(solution)/shard_map/all_to_all | solution.py:143
  78.7 339.4 %all-gather.9.cloned.1.call-start = ((), (), s32[]{:S(2)}) async-start(), calls=%async_computation.9 | async-start | bytes 1351680 | tf_op jit(solution)/shard_map/all_gather | solution.py:159
  336.1 6.1 copy-start.4
  342.2 2.9 copy-start.6
  342.2 2.9 copy-start.8
  342.2 75.9 %copy-start.9 = (s32[256]{0:T(256)S(1)}, s32[256]{0:T(256)}, u32[]{:S(2)}) copy-start(s32[256]{0:T(256)} %param.18) | copy-start | bytes 3076
  342.2 75.9 %copy-start.10 = (bf16[256,640]{1,0:T(8,128)(2,1)S(1)}, bf16[256,640]{1,0:T(8,128)(2,1)}, u32[]{:S(2)}) copy-start(bf16[256,640]{1,0:T(8,128)(2,1)} %param.17) | copy-start | bytes 983044
  344.3 163.4 %copy-start.3 = (bf16[2,32,640]{2,1,0:T(8,128)(2,1)}, bf16[2,32,640]{2,1,0:T(8,128)(2,1)S(1)}, u32[]{:S(2)}) copy-start(bf16[2,32,640]{2,1,0:T(8,128)(2,1)S(1)} %convolution_convert_fusion.2) | copy-start | bytes 245764
  345.0 158.5 %all-gather.5.cloned.1.call-start = ((), (), s32[]{:S(2)}) async-start(), calls=%async_computation.7 | async-start | bytes 8110080 | tf_op jit(solution)/shard_map/all_gather | solution.py:65
  422.0 81.6 %all-to-all-start.4 = ((bf16[8,256,640]{1,2,0:T(8,128)(2,1)}), bf16[8,256,640]{1,2,0:T(8,128)(2,1)S(1)}, u32[]{:S(2)}, u32[]{:S(2)}) async-start(bf16[8,256,640]{1,2,0:T(8,128)(2,1)} %broadcast_in_dim.102), calls=%async_computation.4 | async-start | bytes 5242880 | tf_op jit(solution)/shard_map/all_to_all | solution.py:19
  428.1 150.1 %all-gather.7.cloned.1.call-start = ((), (), s32[]{:S(2)}) async-start(), calls=%async_computation.8 | async-start | bytes 4325376 | tf_op jit(solution)/shard_map/all_gather | solution.py:179
  503.5 19.5 %copy-start.2 = (bf16[8,256,640]{1,2,0:T(8,128)(2,1)}, bf16[8,256,640]{1,2,0:T(8,128)(2,1)S(1)}, u32[]{:S(2)}) copy-start(bf16[8,256,640]{1,2,0:T(8,128)(2,1)S(1)} %all-to-all-done.4) | copy-start | bytes 7864324
  508.8 14.2 %all-to-all-start.5 = ((s32[32,4,1]{1,2,0:T(1,128)}), s32[32,4,1]{1,2,0:T(1,128)S(1)}, u32[]{:S(2)}, u32[]{:S(2)}) async-start(s32[32,4,1]{1,2,0:T(1,128)} %bitcast.31), calls=%async_computation.5 | async-start | bytes 32768 | tf_op jit(solution)/shard_map/all_to_all | solution.py:213
  523.0 20.1 %all-to-all-start.6 = ((bf16[32,4,1280]{2,1,0:T(4,128)(2,1)}), bf16[32,4,1280]{2,1,0:T(4,128)(2,1)S(1)}, u32[]{:S(2)}, u32[]{:S(2)}) async-start(bf16[32,4,1280]{2,1,0:T(4,128)(2,1)} %all_to_all.33), calls=%async_computation.6 | async-start | bytes 655360 | tf_op jit(solution)/shard_map/all_to_all | solution.py:212
  634.7 15.9 %copy-start.1 = (bf16[144,1152]{1,0:T(8,128)(2,1)S(1)}, bf16[144,1152]{1,0:T(8,128)(2,1)}, u32[]{:S(2)}) copy-start(bf16[144,1152]{1,0:T(8,128)(2,1)} %param.14) | copy-start | bytes 995332
Sparse Core Ops, SparseCore 0:
  345.1 72.9 all-gather.8
  420.5 82.9 all-gather.4
  507.9 70.1 all-gather.6
